TPU v7x, 16 devices: a whole 2x2x2 slice. The times are simulated.
16 devices in a mesh: side: 2 (over z), rep: 8 (over y, x, core).
Axes of the slice: x: 2, y: 2, z: 2, core: 2. Of those that a mesh axis runs over, the one named last changes fastest.
Arguments:
- w_up: float32 [2, 6, 896, 4864], P('side', None, 'rep')
- w_down: float32 [2, 6, 4864, 896], P('side', None, None, 'rep')
- g_up: float32 [2, 6, 896, 4864], P('side', None, 'rep')
- g_down: float32 [2, 6, 4864, 896], P('side', None, None, 'rep')
- learn_rate: float32 [], replicated
- prompts: bfloat16 [2, 32768, 896], P('side', 'rep')
- prompt_lens: int32 [8], P('rep')
Outputs:
- output 1: float32 [2, 6, 896, 4864], P('side', None, 'rep')
- output 2: float32 [2, 6, 4864, 896], P('side', None, None, 'rep')
- output 3: bfloat16 [2, 32768, 896], P('side', 'rep')
All inputs are finite; a program needn't handle non-finite values.
Results may differ from a plain program's by a relative error of at most 0.0103396.
Values are sent between devices in bfloat16 or wider.
A program may use at most 1 GiB of HBM per device.

v0:
```python
import jax
import jax.numpy as jnp
from jax import lax
from jax.sharding import PartitionSpec as P


def solution(mesh):
    side_devs = mesh.shape["side"]
    tp_ways = side_devs // 2
    cross_perm = [(src_pos, src_pos + tp_ways) for src_pos in range(tp_ways)]
    up_spec = P("side", None, "rep", None)
    down_spec = P("side", None, None, "rep")
    act_spec = P("side", "rep", None)

    def device_step(w_up, w_down, g_up, g_down, learn_rate, prompts, prompt_lens):
        new_up = w_up - learn_rate * g_up
        new_down = w_down - learn_rate * g_down
        up_sent = lax.ppermute(new_up[0].astype(jnp.bfloat16), "side", cross_perm)
        down_sent = lax.ppermute(new_down[0].astype(jnp.bfloat16), "side", cross_perm)
        up_full = lax.all_gather(up_sent, "rep", axis=1, tiled=True)
        down_full = lax.all_gather(down_sent, "rep", axis=2, tiled=True)
        side_idx = lax.axis_index("side")
        is_gen = side_idx >= tp_ways
        tokens = prompts.shape[1]
        d_piece = prompts.shape[2]
        if tp_ways > 1:
            pieces = lax.all_gather(prompts[0], "side", axis=0)
            hidden = jnp.transpose(pieces[tp_ways:], (1, 0, 2)).reshape(tokens, tp_ways * d_piece)
        else:
            hidden = prompts[0]
        for layer_idx in range(up_full.shape[0]):
            pre_act = jnp.dot(hidden, up_full[layer_idx], preferred_element_type=jnp.float32)
            act_bf = jax.nn.gelu(pre_act, approximate=True).astype(jnp.bfloat16)
            part_sum = jnp.dot(act_bf, down_full[layer_idx], preferred_element_type=jnp.float32)
            if tp_ways > 1:
                part_sum = lax.psum(jnp.where(is_gen, part_sum, 0.0), "side")
            hidden = (hidden.astype(jnp.float32) + part_sum).astype(jnp.bfloat16)
        keep_mask = jnp.arange(tokens)[:, None] < prompt_lens[0]
        tp_idx = jnp.maximum(side_idx - tp_ways, 0)
        own_cols = lax.dynamic_slice_in_dim(hidden, tp_idx * d_piece, d_piece, axis=1)
        out_block = jnp.where(keep_mask & is_gen, own_cols, jnp.zeros_like(own_cols))
        return new_up, new_down, out_block[None]

    mapped = jax.shard_map(
        device_step,
        mesh=mesh,
        in_specs=(up_spec, down_spec, up_spec, down_spec, P(), act_spec, P("rep")),
        out_specs=(up_spec, down_spec, act_spec),
        check_vma=False,
    )
    return mapped
```

profile of v0, /device:TPU:0, one launch (start us, length us, event | category | flops | bytes accessed | tf_op | source)
XLA Modules:
  0.0 1289.0 jit_solution(18078376530039216666)
XLA Ops:
  7.2 0.0 all-gather.3.cloned.1.call-start
  7.9 14.4 %convert_bitcast_fusion.1 = (bf16[6,112,4864]{2,1,0:T(8,128)(2,1)S(1)}, f32[1,6,112,4864]{3,2,1,0:T(8,128)}) fusion(f32[1,6,112,4864]{3,2,1,0:T(8,128)} %param.7, f32[1,6,112,4864]{3,2,1,0:T(8,128)} %param.9, f32[]{:T(128)S(6)} %copy.40), kind=kLoop, calls=%fused_computation.77 | loop fusion | flops 9805824 | bytes 45760516 | tf_op jit(solution)/shard_map/convert_element_type | solution.py:18
  22.3 8.0 collective-permute-start
  30.3 137.2 %collective-permute-done = bf16[6,112,4864]{2,1,0:T(8,128)(2,1)} collective-permute-done((bf16[6,112,4864]{2,1,0:T(8,128)(2,1)S(1)}, bf16[6,112,4864]{2,1,0:T(8,128)(2,1)}, u32[]{:S(2)}, u32[]{:S(2)}) %collective-permute-start) | collective-permute-done | bytes 6537248 | tf_op jit(solution)/shard_map/ppermute | solution.py:18
  167.5 0.0 all-gather.3.cloned.1.call-update
  167.5 0.0 all-gather.5.cloned.1.call-start
  167.6 14.4 %convert_bitcast_fusion = (bf16[6,4864,112]{1,2,0:T(8,128)(2,1)S(1)}, f32[1,6,4864,112]{2,3,1,0:T(8,128)}) fusion(f32[1,6,4864,112]{2,3,1,0:T(8,128)} %param.8, f32[1,6,4864,112]{2,3,1,0:T(8,128)} %param.10, f32[]{:T(128)S(6)} %copy.40), kind=kLoop, calls=%fused_computation.76 | loop fusion | flops 9805824 | bytes 45760516 | tf_op jit(solution)/shard_map/convert_element_type | solution.py:19
  182.0 7.1 collective-permute-start.1
  189.1 136.6 %collective-permute-done.1 = bf16[6,4864,112]{1,2,0:T(8,128)(2,1)} collective-permute-done((bf16[6,4864,112]{1,2,0:T(8,128)(2,1)S(1)}, bf16[6,4864,112]{1,2,0:T(8,128)(2,1)}, u32[]{:S(2)}, u32[]{:S(2)}) %collective-permute-start.1) | collective-permute-done | bytes 6537248 | tf_op jit(solution)/shard_map/ppermute | solution.py:19
  325.6 0.0 all-gather.5.cloned.1.call-update
  326.3 0.6 fusion.49
  326.9 79.2 %all-gather.3.cloned.1.call-done = bf16[6,896,4864]{2,1,0:T(8,128)(2,1)} async-done(((bf16[6,112,4864]{2,1,0:T(8,128)(2,1)}), bf16[6,896,4864]{2,1,0:T(8,128)(2,1)}) %all-gather.3.cloned.1.call-update) | async-done | bytes 52297744 | tf_op jit(solution)/shard_map/all_gather | solution.py:20
  406.1 67.2 %fusion.7 = bf16[4096,4864]{0,1:T(8,128)(2,1)} fusion(bf16[6,896,4864]{2,1,0:T(8,128)(2,1)} %all-gather.3.cloned.1.call-done, bf16[1,4096,896]{2,1,0:T(8,128)(2,1)} %param.12), kind=kOutput, calls=%fused_computation.13 | convolution fusion | flops 35881222144 | bytes 55902208 | tf_op jit(solution)/shard_map/dot_general | solution.py:32
  473.3 171.2 %all-gather.5.cloned.1.call-done = bf16[6,4864,896]{1,2,0:T(8,128)(2,1)} async-done(((bf16[6,4864,112]{1,2,0:T(8,128)(2,1)}), bf16[6,4864,896]{1,2,0:T(8,128)(2,1)}) %all-gather.5.cloned.1.call-update) | async-done | bytes 52297744 | tf_op jit(solution)/shard_map/all_gather | solution.py:21
  644.5 49.8 %add_convert_fusion.5 = bf16[4096,896]{1,0:T(8,128)(2,1)} fusion(bf16[4096,4864]{0,1:T(8,128)(2,1)} %fusion.7, bf16[6,4864,896]{1,2,0:T(8,128)(2,1)} %all-gather.5.cloned.1.call-done, bf16[1,4096,896]{2,1,0:T(8,128)(2,1)} %param.12), kind=kOutput, calls=%fused_computation.59 | convolution fusion | flops 35712925696 | bytes 63242240 | tf_op jit(solution)/shard_map/dot_general | solution.py:34
  694.3 67.3 %fusion.15 = bf16[4096,4864]{0,1:T(8,128)(2,1)} fusion(bf16[4096,896]{1,0:T(8,128)(2,1)} %add_convert_fusion.5, bf16[6,896,4864]{2,1,0:T(8,128)(2,1)} %all-gather.3.cloned.1.call-done), kind=kOutput, calls=%fused_computation.21 | convolution fusion | flops 35881222144 | bytes 55902208 | tf_op jit(solution)/shard_map/dot_general | solution.py:32
  761.6 49.5 %add_convert_fusion.4 = bf16[4096,896]{1,0:T(8,128)(2,1)} fusion(bf16[4096,896]{1,0:T(8,128)(2,1)} %add_convert_fusion.5, bf16[4096,4864]{0,1:T(8,128)(2,1)} %fusion.15, bf16[6,4864,896]{1,2,0:T(8,128)(2,1)} %all-gather.5.cloned.1.call-done), kind=kOutput, calls=%fused_computation.58 | convolution fusion | flops 35712925696 | bytes 63242240 | tf_op jit(solution)/shard_map/dot_general | solution.py:34
  811.1 67.5 %fusion.23 = bf16[4096,4864]{0,1:T(8,128)(2,1)} fusion(bf16[4096,896]{1,0:T(8,128)(2,1)} %add_convert_fusion.4, bf16[6,896,4864]{2,1,0:T(8,128)(2,1)} %all-gather.3.cloned.1.call-done), kind=kOutput, calls=%fused_computation.29 | convolution fusion | flops 35881222144 | bytes 55902208 | tf_op jit(solution)/shard_map/dot_general | solution.py:32
  878.6 49.6 %add_convert_fusion.3 = bf16[4096,896]{1,0:T(8,128)(2,1)} fusion(bf16[4096,896]{1,0:T(8,128)(2,1)} %add_convert_fusion.4, bf16[4096,4864]{0,1:T(8,128)(2,1)} %fusion.23, bf16[6,4864,896]{1,2,0:T(8,128)(2,1)} %all-gather.5.cloned.1.call-done), kind=kOutput, calls=%fused_computation.57 | convolution fusion | flops 35712925696 | bytes 63242240 | tf_op jit(solution)/shard_map/dot_general | solution.py:34
  928.2 67.6 %fusion.31 = bf16[4096,4864]{0,1:T(8,128)(2,1)} fusion(bf16[4096,896]{1,0:T(8,128)(2,1)} %add_convert_fusion.3, bf16[6,896,4864]{2,1,0:T(8,128)(2,1)} %all-gather.3.cloned.1.call-done), kind=kOutput, calls=%fused_computation.37 | convolution fusion | flops 35881222144 | bytes 55902208 | tf_op jit(solution)/shard_map/dot_general | solution.py:32
  995.7 49.8 %add_convert_fusion.2 = bf16[4096,896]{1,0:T(8,128)(2,1)} fusion(bf16[4096,896]{1,0:T(8,128)(2,1)} %add_convert_fusion.3, bf16[4096,4864]{0,1:T(8,128)(2,1)} %fusion.31, bf16[6,4864,896]{1,2,0:T(8,128)(2,1)} %all-gather.5.cloned.1.call-done), kind=kOutput, calls=%fused_computation.56 | convolution fusion | flops 35712925696 | bytes 63242240 | tf_op jit(solution)/shard_map/dot_general | solution.py:34
  1045.6 67.5 %fusion.39 = bf16[4096,4864]{0,1:T(8,128)(2,1)} fusion(bf16[4096,896]{1,0:T(8,128)(2,1)} %add_convert_fusion.2, bf16[6,896,4864]{2,1,0:T(8,128)(2,1)} %all-gather.3.cloned.1.call-done), kind=kOutput, calls=%fused_computation.45 | convolution fusion | flops 35881222144 | bytes 55902208 | tf_op jit(solution)/shard_map/dot_general | solution.py:32
  1113.0 49.5 %add_convert_fusion.1 = bf16[4096,896]{1,0:T(8,128)(2,1)} fusion(bf16[4096,896]{1,0:T(8,128)(2,1)} %add_convert_fusion.2, bf16[4096,4864]{0,1:T(8,128)(2,1)} %fusion.39, bf16[6,4864,896]{1,2,0:T(8,128)(2,1)} %all-gather.5.cloned.1.call-done), kind=kOutput, calls=%fused_computation.55 | convolution fusion | flops 35712925696 | bytes 63242240 | tf_op jit(solution)/shard_map/dot_general | solution.py:34
  1162.6 0.0 copy-start
  1162.6 67.6 %fusion.47 = bf16[4096,4864]{0,1:T(8,128)(2,1)} fusion(bf16[4096,896]{1,0:T(8,128)(2,1)} %add_convert_fusion.1, bf16[6,896,4864]{2,1,0:T(8,128)(2,1)} %all-gather.3.cloned.1.call-done), kind=kOutput, calls=%fused_computation.53 | convolution fusion | flops 35881222144 | bytes 55902208 | tf_op jit(solution)/shard_map/dot_general | solution.py:32
  1230.1 0.0 copy-done
  1230.1 51.6 %select_bitcast_fusion = bf16[1,4096,896]{2,1,0:T(8,128)(2,1)} fusion(pred[4096]{0:T(1024)(128)(4,1)S(1)} %copy-done, bf16[4096,4864]{0,1:T(8,128)(2,1)} %fusion.47, bf16[6,4864,896]{1,2,0:T(8,128)(2,1)} %all-gather.5.cloned.1.call-done, bf16[4096,896]{1,0:T(8,128)(2,1)} %add_convert_fusion.1), kind=kOutput, calls=%fused_computation.75 | convolution fusion | flops 35716595712 | bytes 63246336 | tf_op jit(solution)/shard_map/dot_general | solution.py:34
Async XLA Ops:
  7.2 399.0 %all-gather.3.cloned.1.call-start = ((), (), s32[]{:S(2)}) async-start(), calls=%async_computation | async-start | bytes 58834944 | tf_op jit(solution)/shard_map/all_gather | solution.py:20
  22.3 145.2 %collective-permute-start = (bf16[6,112,4864]{2,1,0:T(8,128)(2,1)S(1)}, bf16[6,112,4864]{2,1,0:T(8,128)(2,1)}, u32[]{:S(2)}, u32[]{:S(2)}) collective-permute-start(bf16[6,112,4864]{2,1,0:T(8,128)(2,1)S(1)} %get-tuple-element.5), channel_id=1, source_target_pairs={{0,8},{1,9},{2,10},{3,11},{4,12},{5,13},{6,14},{7,15}} | collective-permute-start | bytes 19611656 | tf_op jit(solution)/shard_map/ppermute | solution.py:18
  167.5 477.0 %all-gather.5.cloned.1.call-start = ((), (), s32[]{:S(2)}) async-start(), calls=%async_computation.1 | async-start | bytes 58834944 | tf_op jit(solution)/shard_map/all_gather | solution.py:21
  182.0 143.7 %collective-permute-start.1 = (bf16[6,4864,112]{1,2,0:T(8,128)(2,1)S(1)}, bf16[6,4864,112]{1,2,0:T(8,128)(2,1)}, u32[]{:S(2)}, u32[]{:S(2)}) collective-permute-start(bf16[6,4864,112]{1,2,0:T(8,128)(2,1)S(1)} %get-tuple-element.3), channel_id=1, source_target_pairs={{0,8},{1,9},{2,10},{3,11},{4,12},{5,13},{6,14},{7,15}} | collective-permute-start | bytes 19611656 | tf_op jit(solution)/shard_map/ppermute | solution.py:19
  1162.6 67.6 %copy-start = (pred[4096]{0:T(1024)(128)(4,1)S(1)}, pred[4096]{0:T(1024)(128)(4,1)}, u32[]{:S(2)}) copy-start(pred[4096]{0:T(1024)(128)(4,1)} %fusion.49) | copy-start | bytes 12292
Sparse Core Ops, SparseCore 0:
  167.6 238.4 all-gather.2
  408.0 236.4 all-gather.4
where the time goes:
time: 1300 us; the launch traced here: 1290 us
  matrix products  704 us (54%)
  waiting for transfers between devices  524 us (40%)
  other arithmetic  29.5 us (2%)
  between operations  15.8 us (1%)
  starting transfers between devices  15.1 us (1%)
    dot_general x6, matrix products, device_step(): jnp.dot(hidden, up_full[layer_idx], preferred_element_type=jnp.float32)  405 us
    dot_general x6, matrix products, device_step(): jnp.dot(act_bf, down_full[layer_idx], preferred_element_type=jnp.float32)  300 us
    all_gather x1, waiting for transfers between devices, device_step(): down_full = lax.all_gather(down_sent, 'rep', axis=2, tiled=True)  171 us
    ppermute x1, waiting for transfers between devices, device_step(): up_sent = lax.ppermute(new_up[0].astype(jnp.bfloat16), 'side', cross_perm)  137 us
    ppermute x1, waiting for transfers between devices, device_step(): lax.ppermute(new_down[0].astype(jnp.bfloat16), 'side', cross_perm)  137 us
    all_gather x1, waiting for transfers between devices, device_step(): up_full = lax.all_gather(up_sent, 'rep', axis=1, tiled=True)  79.2 us
  transfers between devices with their start and end apart: 4, of which 4 were waited for; matrix products, arithmetic and copies ran while one was open for 6% of the time, Pallas kernels for 0%

commit v1 on v0

v1 whole, which is shorter than its diff:
```python
import functools

import jax
import jax.numpy as jnp
from jax import lax
from jax.experimental import pallas as pl
from jax.experimental.pallas import tpu as pltpu
from jax.sharding import PartitionSpec as P

ROOT_2_PI = 0.7978845608
CUBIC = 0.044715 * ROOT_2_PI


def gelu(z):
    half = 0.5 * z
    return half + half * jnp.tanh(z * (ROOT_2_PI + CUBIC * (z * z)))


def cuts(total, step):
    return [(at, min(step, total - at)) for at in range(0, total, step)]


def layer_kernel(h_ref, up_ref, down_ref, out_ref, act_ref):
    width = h_ref.shape[1]
    for at, size in cuts(up_ref.shape[1], 512):
        z = jnp.dot(h_ref[...], up_ref[:, at : at + size], preferred_element_type=jnp.float32)
        act_ref[:, at : at + size] = gelu(z).astype(jnp.bfloat16)
    for at, size in cuts(width, 256):
        p = lax.dot_general(
            act_ref[...], down_ref[at : at + size, :], (((1,), (1,)), ((), ())), preferred_element_type=jnp.float32
        )
        out_ref[:, at : at + size] = (h_ref[:, at : at + size].astype(jnp.float32) + p).astype(jnp.bfloat16)


def mlp_layer(h, weights):
    rows, width = h.shape
    ffn = weights.shape[2]
    block = 512

    def matrix(which):
        return pl.BlockSpec((pl.Squeezed(), width, ffn), lambda i: (which, 0, 0), pipeline_mode=pl.Buffered(1))

    return pl.pallas_call(
        layer_kernel,
        grid=(rows // block,),
        in_specs=[pl.BlockSpec((block, width), lambda i: (i, 0)), matrix(0), matrix(1)],
        out_specs=pl.BlockSpec((block, width), lambda i: (i, 0)),
        out_shape=jax.ShapeDtypeStruct((rows, width), jnp.bfloat16),
        scratch_shapes=[pltpu.VMEM((block, ffn), jnp.bfloat16)],
        compiler_params=pltpu.CompilerParams(vmem_limit_bytes=48 * 2**20),
        cost_estimate=pl.CostEstimate(
            flops=4 * rows * width * ffn, bytes_accessed=4 * (rows + ffn) * width, transcendentals=rows * ffn
        ),
        name="mlp_layer",
    )(h, weights, weights)


def solution(mesh):
    up_spec = P("side", None, "rep", None)
    down_spec = P("side", None, None, "rep")
    act_spec = P("side", "rep", None)

    def device_step(w_up, w_down, g_up, g_down, learn_rate, prompts, prompt_lens):
        is_gen = lax.axis_index("side") == 1
        layers = w_up.shape[1]
        tokens = prompts.shape[1]
        half = tokens // 2
        new_up = w_up - learn_rate * g_up
        new_down = w_down - learn_rate * g_down
        up_bf = new_up[0].astype(jnp.bfloat16)
        down_bf = jnp.swapaxes(new_down[0], 1, 2).astype(jnp.bfloat16)
        own = [jnp.stack([up_bf[layer], down_bf[layer]]) for layer in range(layers)]
        moved = lax.ppermute(prompts[0, half:], "side", [(1, 0)])
        hidden = jnp.where(is_gen, prompts[0, :half], moved)

        def cross(own):
            return jnp.where(is_gen, lax.ppermute(own, "side", [(0, 1)]), own)

        def gather(staged):
            return lax.all_gather(staged, "rep", axis=1, tiled=True)

        staged = [cross(own[0]), cross(own[1]), cross(own[2])]
        gathered = [gather(staged[0]), gather(staged[1])]
        for layer in range(layers):
            hidden = mlp_layer(hidden, gathered[layer])
            if layer + 2 < layers:
                later = own[min(layer + 3, layers - 1)]
                hidden, ready, later = lax.optimization_barrier((hidden, staged[layer + 2], later))
                gathered.append(gather(ready))
                if layer + 3 < layers:
                    staged.append(cross(later))
        back = lax.ppermute(hidden, "side", [(0, 1)])
        out = jnp.concatenate([hidden, back], axis=0)
        keep = (jnp.arange(tokens)[:, None] < prompt_lens[0]) & is_gen
        out = jnp.where(keep, out, jnp.zeros_like(out))
        return new_up, new_down, out[None]

    return jax.shard_map(
        device_step,
        mesh=mesh,
        in_specs=(up_spec, down_spec, up_spec, down_spec, P(), act_spec, P("rep")),
        out_specs=(up_spec, down_spec, act_spec),
        check_vma=False,
    )
```

time: 1300 us -> 803 us (0.62)
  matrix products: 704 us -> 0 us
  Pallas kernels: 0 us -> 295 us
  waiting for transfers between devices: 524 us -> 373 us
  other arithmetic: 29.5 us -> 58.1 us
  local copies, waits for them, and re-layouts: 0.01 us -> 24.2 us
  starting transfers between devices: 15.1 us -> 33.1 us
    dot_general x12 -> x0, matrix products: 704 us -> none  [the longest x6 405 us: device_step(): jnp.dot(hidden, up_full[layer_idx], preferred_element_type=jnp.float32)]
    pallas_call x0 -> x6, Pallas kernels: none -> 295 us  [mlp_layer(): pl.pallas_call(layer_kernel, grid=(rows // block,), in_specs=[pl.BlockSpe...]
    all_gather x2 -> x6, waiting for transfers between devices: 250 us -> 48.3 us  [gather(): return lax.all_gather(staged, 'rep', axis=1, tiled=True)]
    ppermute x2 -> x8, waiting for transfers between devices: 274 us -> 324 us  [the longest x6 219 us: cross(): return jnp.where(is_gen, lax.ppermute(own, 'side', [(0, 1)]), own)]
    select_n x0 -> x8, other arithmetic: none -> 21.9 us  [the longest x6 11.1 us: cross(): return jnp.where(is_gen, lax.ppermute(own, 'side', [(0, 1)]), own)]
    ppermute x2 -> x8, starting transfers between devices: 15.1 us -> 32.9 us  [the longest x6 28 us: cross(): return jnp.where(is_gen, lax.ppermute(own, 'side', [(0, 1)]), own)]
    unnamed x2 -> x32, local copies, waits for them, and re-layouts: 0.01 us -> 16.1 us
  transfers between devices with their start and end apart: 4 -> 14, of which waited for: 4 -> 9; matrix products, arithmetic and copies ran while one was open for 6% -> 3% of each run, Pallas kernels for 0% -> 31%
where the time goes in v1:
time: 803 us; the launch traced here: 799 us
  waiting for transfers between devices  373 us (46%)
  Pallas kernels  295 us (37%)
  other arithmetic  58.1 us (7%)
  starting transfers between devices  33.1 us (4%)
  local copies, waits for them, and re-layouts  24.2 us (3%)
  between operations  15.9 us (2%)
    pallas_call x6, Pallas kernels, mlp_layer(): pl.pallas_call(layer_kernel, grid=(rows // block,), in_specs=[pl.BlockSpe...  295 us
    ppermute x6, waiting for transfers between devices, cross(): return jnp.where(is_gen, lax.ppermute(own, 'side', [(0, 1)]), own)  219 us
    ppermute x1, waiting for transfers between devices, device_step(): back = lax.ppermute(hidden, 'side', [(0, 1)])  78.1 us
    all_gather x6, waiting for transfers between devices, gather(): return lax.all_gather(staged, 'rep', axis=1, tiled=True)  48.3 us
    ppermute x6, starting transfers between devices, cross(): return jnp.where(is_gen, lax.ppermute(own, 'side', [(0, 1)]), own)  28 us
    ppermute x1, waiting for transfers between devices, device_step(): moved = lax.ppermute(prompts[0, half:], 'side', [(1, 0)])  27 us
    unnamed x32, local copies, waits for them, and re-layouts  16.1 us
  transfers between devices with their start and end apart: 14, of which 9 were waited for; matrix products, arithmetic and copies ran while one was open for 3% of the time, Pallas kernels for 31%

profile of v1, /device:TPU:0, one launch (start us, length us, event | category | flops | bytes accessed | tf_op | source)
XLA Modules:
  0.0 798.7 jit_solution(10380667277678057996)
XLA Ops:
  7.2 0.0 all-gather.7.cloned.1.call-start
  7.9 14.4 %convert_bitcast_fusion = (bf16[6,112,4864]{2,1,0:T(8,128)(2,1)S(1)}, f32[1,6,4864,112]{2,3,1,0:T(8,128)}) fusion(f32[1,6,4864,112]{2,3,1,0:T(8,128)} %param.8, f32[1,6,4864,112]{2,3,1,0:T(8,128)} %param.10, f32[]{:T(128)S(6)} %copy.10), kind=kLoop, calls=%fused_computation.3 | loop fusion | flops 9805824 | bytes 45760516 | tf_op jit(solution)/shard_map/convert_element_type | solution.py:71
  22.3 1.7 fusion.2
  24.0 4.1 copy-done.5
  28.2 11.2 %fusion.1 = (bf16[1,6,112,4864]{3,2,1,0:T(8,128)(2,1)S(1)}, f32[1,6,112,4864]{3,2,1,0:T(8,128)}) fusion(f32[1,6,112,4864]{3,2,1,0:T(8,128)S(1)} %copy-done.5, f32[1,6,112,4864]{3,2,1,0:T(8,128)} %param.9, f32[]{:T(128)S(6)} %copy.10), kind=kLoop, calls=%fused_computation.26 | loop fusion | flops 9805824 | bytes 45760516 | tf_op jit(solution)/shard_map/convert_element_type | solution.py:70
  39.3 2.2 slice_bitcast_fusion.1
  41.5 1.7 pad_maximum_fusion
  43.2 0.0 copy-done.8
  43.2 6.6 collective-permute-start.1
  49.8 45.2 %collective-permute-done.1 = bf16[2,112,4864]{2,1,0:T(8,128)(2,1)} collective-permute-done((bf16[2,112,4864]{2,1,0:T(8,128)(2,1)}, bf16[2,112,4864]{2,1,0:T(8,128)(2,1)}, u32[]{:S(2)}, u32[]{:S(2)}) %collective-permute-start.1) | collective-permute-done | bytes 2179104 | tf_op jit(solution)/shard_map/ppermute | solution.py:77
  95.0 3.1 broadcast_select_fusion.5
  98.2 0.0 all-gather.7.cloned.1.call-update
  98.2 0.0 all-gather.9.cloned.1.call-start
  98.2 1.5 pad_maximum_fusion.3
  99.8 5.2 collective-permute-start.3
  105.0 45.7 %collective-permute-done.3 = bf16[2,112,4864]{2,1,0:T(8,128)(2,1)S(1)} collective-permute-done((bf16[2,112,4864]{2,1,0:T(8,128)(2,1)S(1)}, bf16[2,112,4864]{2,1,0:T(8,128)(2,1)S(1)}, u32[]{:S(2)}, u32[]{:S(2)}) %collective-permute-start.3) | collective-permute-done | bytes 2179104 | tf_op jit(solution)/shard_map/ppermute | solution.py:77
  150.7 1.7 broadcast_select_fusion.3
  152.4 0.0 all-gather.9.cloned.1.call-update
  152.4 0.0 all-gather.11.cloned.1.call-start
  152.5 4.2 slice_bitcast_fusion
  156.6 1.3 collective-permute-start
  157.9 0.2 pad_maximum_fusion.1
  158.1 6.8 collective-permute-start.2
  165.0 1.6 pad_maximum_fusion.2
  166.6 43.0 %collective-permute-done.2 = bf16[2,112,4864]{2,1,0:T(8,128)(2,1)S(1)} collective-permute-done((bf16[2,112,4864]{2,1,0:T(8,128)(2,1)S(1)}, bf16[2,112,4864]{2,1,0:T(8,128)(2,1)S(1)}, u32[]{:S(2)}, u32[]{:S(2)}) %collective-permute-start.2) | collective-permute-done | bytes 2179104 | tf_op jit(solution)/shard_map/ppermute | solution.py:77
  209.6 1.6 broadcast_select_fusion.4
  211.2 27.0 %collective-permute-done = bf16[2048,896]{1,0:T(8,128)(2,1)} collective-permute-done((bf16[2048,896]{1,0:T(8,128)(2,1)}, bf16[2048,896]{1,0:T(8,128)(2,1)}, u32[]{:S(2)}, u32[]{:S(2)}) %collective-permute-start) | collective-permute-done | bytes 3670048 | tf_op jit(solution)/shard_map/ppermute | solution.py:73
  238.2 5.4 bitcast_select_fusion.h_ref
  243.6 49.0 %mlp_layer.6.h_ref = bf16[2048,896]{1,0:T(8,128)(2,1)S(1)} custom-call(bf16[2048,896]{1,0:T(8,128)(2,1)} %bitcast_select_fusion.h_ref, bf16[2,896,4864]{2,1,0:T(8,128)(2,1)} %all-gather.7.cloned.1.call-done.up_ref.down_ref, bf16[2,896,4864]{2,1,0:T(8,128)(2,1)} %all-gather.7.cloned.1.call-done.up_ref.down_ref), custom_call_target="tpu_custom_call" | custom-call | flops 35701915648 | bytes 24772608 | tf_op jit(solution)/shard_map/mlp_layer/pallas_call | solution.py:43
  292.7 1.8 copy-done.2
  294.5 0.0 all-gather.11.cloned.1.call-update
  294.5 0.0 all-gather.13.cloned.1.call-start
  294.6 1.2 copy-done.13
  295.7 2.9 pad_maximum_fusion.4
  298.6 2.9 collective-permute-start.4
  301.5 0.0 all-gather.9.cloned.1.call-done.up_ref.down_ref
  301.5 49.0 %mlp_layer.7.h_ref = bf16[2048,896]{1,0:T(8,128)(2,1)S(1)} custom-call(bf16[2048,896]{1,0:T(8,128)(2,1)} %copy-done.2, bf16[2,896,4864]{2,1,0:T(8,128)(2,1)} %all-gather.9.cloned.1.call-done.up_ref.down_ref, bf16[2,896,4864]{2,1,0:T(8,128)(2,1)} %all-gather.9.cloned.1.call-done.up_ref.down_ref), custom_call_target="tpu_custom_call" | custom-call | flops 35701915648 | bytes 24772608 | tf_op jit(solution)/shard_map/mlp_layer/pallas_call | solution.py:43
  350.6 1.8 copy-done
  352.4 1.6 broadcast_select_fusion.2
  354.1 0.0 all-gather.13.cloned.1.call-update
  354.1 0.0 all-gather.15.cloned.1.call-start
  354.1 1.5 copy-done.10
  355.7 1.8 collective-permute-start.5
  357.5 2.7 pad_maximum_fusion.5
  360.3 41.5 %collective-permute-done.5 = bf16[2,112,4864]{2,1,0:T(8,128)(2,1)S(1)} collective-permute-done((bf16[2,112,4864]{2,1,0:T(8,128)(2,1)S(1)}, bf16[2,112,4864]{2,1,0:T(8,128)(2,1)S(1)}, u32[]{:S(2)}, u32[]{:S(2)}) %collective-permute-start.5) | collective-permute-done | bytes 2179104 | tf_op jit(solution)/shard_map/ppermute | solution.py:77
  401.8 1.6 broadcast_select_fusion.1
  403.3 49.2 %mlp_layer.8.h_ref = bf16[2048,896]{1,0:T(8,128)(2,1)S(1)} custom-call(bf16[2048,896]{1,0:T(8,128)(2,1)} %copy-done, bf16[2,896,4864]{2,1,0:T(8,128)(2,1)} %all-gather.11.cloned.1.call-done.up_ref.down_ref, bf16[2,896,4864]{2,1,0:T(8,128)(2,1)} %all-gather.11.cloned.1.call-done.up_ref.down_ref), custom_call_target="tpu_custom_call" | custom-call | flops 35701915648 | bytes 24772608 | tf_op jit(solution)/shard_map/mlp_layer/pallas_call | solution.py:43
  452.5 1.8 copy-done.1
  454.3 0.0 all-gather.15.cloned.1.call-update
  454.4 0.0 all-gather.17.cloned.1.call-start
  454.4 4.7 collective-permute-start.6
  459.1 43.7 %collective-permute-done.6 = bf16[2,112,4864]{2,1,0:T(8,128)(2,1)S(1)} collective-permute-done((bf16[2,112,4864]{2,1,0:T(8,128)(2,1)S(1)}, bf16[2,112,4864]{2,1,0:T(8,128)(2,1)S(1)}, u32[]{:S(2)}, u32[]{:S(2)}) %collective-permute-start.6) | collective-permute-done | bytes 2179104 | tf_op jit(solution)/shard_map/ppermute | solution.py:77
  502.9 1.5 broadcast_select_fusion
  504.4 49.0 %mlp_layer.9.h_ref = bf16[2048,896]{1,0:T(8,128)(2,1)S(1)} custom-call(bf16[2048,896]{1,0:T(8,128)(2,1)} %copy-done.1, bf16[2,896,4864]{2,1,0:T(8,128)(2,1)} %all-gather.13.cloned.1.call-done.up_ref.down_ref, bf16[2,896,4864]{2,1,0:T(8,128)(2,1)} %all-gather.13.cloned.1.call-done.up_ref.down_ref), custom_call_target="tpu_custom_call" | custom-call | flops 35701915648 | bytes 24772608 | tf_op jit(solution)/shard_map/mlp_layer/pallas_call | solution.py:43
  553.5 1.8 copy-done.3
  555.3 0.0 all-gather.17.cloned.1.call-update
  555.3 8.9 %all-gather.15.cloned.1.call-done.up_ref.down_ref = bf16[2,896,4864]{2,1,0:T(8,128)(2,1)} async-done(((bf16[2,112,4864]{2,1,0:T(8,128)(2,1)}), bf16[2,896,4864]{2,1,0:T(8,128)(2,1)}) %all-gather.15.cloned.1.call-update) | async-done | bytes 17432592 | tf_op jit(solution)/shard_map/all_gather | solution.py:80
  564.2 49.2 %mlp_layer.10.h_ref = bf16[2048,896]{1,0:T(8,128)(2,1)S(1)} custom-call(bf16[2048,896]{1,0:T(8,128)(2,1)} %copy-done.3, bf16[2,896,4864]{2,1,0:T(8,128)(2,1)} %all-gather.15.cloned.1.call-done.up_ref.down_ref, bf16[2,896,4864]{2,1,0:T(8,128)(2,1)} %all-gather.15.cloned.1.call-done.up_ref.down_ref), custom_call_target="tpu_custom_call" | custom-call | flops 35701915648 | bytes 24772608 | tf_op jit(solution)/shard_map/mlp_layer/pallas_call | solution.py:43
  613.5 1.8 copy-done.4
  615.3 39.3 %all-gather.17.cloned.1.call-done.up_ref.down_ref = bf16[2,896,4864]{2,1,0:T(8,128)(2,1)} async-done(((bf16[2,112,4864]{2,1,0:T(8,128)(2,1)}), bf16[2,896,4864]{2,1,0:T(8,128)(2,1)}) %all-gather.17.cloned.1.call-update) | async-done | bytes 17432592 | tf_op jit(solution)/shard_map/all_gather | solution.py:80
  654.6 49.3 %mlp_layer.11 = bf16[2048,896]{1,0:T(8,128)(2,1)S(1)} custom-call(bf16[2048,896]{1,0:T(8,128)(2,1)} %copy-done.4, bf16[2,896,4864]{2,1,0:T(8,128)(2,1)} %all-gather.17.cloned.1.call-done.up_ref.down_ref, bf16[2,896,4864]{2,1,0:T(8,128)(2,1)} %all-gather.17.cloned.1.call-done.up_ref.down_ref), custom_call_target="tpu_custom_call" | custom-call | flops 35701915648 | bytes 24772608 | tf_op jit(solution)/shard_map/mlp_layer/pallas_call | solution.py:43
  703.9 3.6 collective-permute-start.7
  708.2 78.1 %collective-permute-done.7 = bf16[2048,896]{1,0:T(8,128)(2,1)S(1)} collective-permute-done((bf16[2048,896]{1,0:T(8,128)(2,1)S(1)}, bf16[2048,896]{1,0:T(8,128)(2,1)S(1)}, u32[]{:S(2)}, u32[]{:S(2)}) %collective-permute-start.7) | collective-permute-done | bytes 3670048 | tf_op jit(solution)/shard_map/ppermute | solution.py:92
  786.3 5.3 maximum_select_fusion
  (28 shorter events, 0.1 us)
Async XLA Ops:
  7.2 236.5 %all-gather.7.cloned.1.call-start = ((), (), s32[]{:S(2)}) async-start(), calls=%async_computation | async-start | bytes 19611648 | tf_op jit(solution)/shard_map/all_gather | solution.py:80
  22.3 5.9 copy-start.5
  28.2 13.3 %copy-start.7 = (bf16[1,112,4864]{2,1,0:T(8,128)(2,1)}, bf16[1,112,4864]{2,1,0:T(8,128)(2,1)S(1)}, u32[]{:S(2)}) copy-start(bf16[1,112,4864]{2,1,0:T(8,128)(2,1)S(1)} %get-tuple-element.40) | copy-start | bytes 3268612
  41.5 1.7 copy-start.8
  43.2 51.8 %collective-permute-start.1 = (bf16[2,112,4864]{2,1,0:T(8,128)(2,1)}, bf16[2,112,4864]{2,1,0:T(8,128)(2,1)}, u32[]{:S(2)}, u32[]{:S(2)}) collective-permute-start(bf16[2,112,4864]{2,1,0:T(8,128)(2,1)} %pad_maximum_fusion), channel_id=1, source_target_pairs={{0,8},{1,9},{2,10},{3,11},{4,12},{5,13},{6,14},{7,15}} | collective-permute-start | bytes 6537224 | tf_op jit(solution)/shard_map/ppermute | solution.py:77
  98.2 203.4 %all-gather.9.cloned.1.call-start = ((), (), s32[]{:S(2)}) async-start(), calls=%async_computation.1 | async-start | bytes 19611648 | tf_op jit(solution)/shard_map/all_gather | solution.py:80
  98.2 52.5 %copy-start.6 = (bf16[1,112,4864]{2,1,0:T(8,128)(2,1)S(1)}, bf16[1,112,4864]{2,1,0:T(8,128)(2,1)}, u32[]{:S(2)}) copy-start(bf16[1,112,4864]{2,1,0:T(8,128)(2,1)} %get-tuple-element.31) | copy-start | bytes 3268612
  99.8 50.9 %collective-permute-start.3 = (bf16[2,112,4864]{2,1,0:T(8,128)(2,1)S(1)}, bf16[2,112,4864]{2,1,0:T(8,128)(2,1)S(1)}, u32[]{:S(2)}, u32[]{:S(2)}) collective-permute-start(bf16[2,112,4864]{2,1,0:T(8,128)(2,1)S(1)} %pad_maximum_fusion.3), channel_id=1, source_target_pairs={{0,8},{1,9},{2,10},{3,11},{4,12},{5,13},{6,14},{7,15}} | collective-permute-start | bytes 6537224 | tf_op jit(solution)/shard_map/ppermute | solution.py:77
  152.4 250.9 %all-gather.11.cloned.1.call-start = ((), (), s32[]{:S(2)}) async-start(), calls=%async_computation.2 | async-start | bytes 19611648 | tf_op jit(solution)/shard_map/all_gather | solution.py:80
  156.6 81.6 %collective-permute-start = (bf16[2048,896]{1,0:T(8,128)(2,1)}, bf16[2048,896]{1,0:T(8,128)(2,1)}, u32[]{:S(2)}, u32[]{:S(2)}) collective-permute-start(bf16[2048,896]{1,0:T(8,128)(2,1)} %slice_bitcast_fusion), channel_id=1, source_target_pairs={{8,0},{9,1},{10,2},{11,3},{12,4},{13,5},{14,6},{15,7}} | collective-permute-start | bytes 11010056 | tf_op jit(solution)/shard_map/ppermute | solution.py:73
  157.9 7.0 copy-start.14
  157.9 7.0 copy-start.15
  158.1 51.5 %collective-permute-start.2 = (bf16[2,112,4864]{2,1,0:T(8,128)(2,1)S(1)}, bf16[2,112,4864]{2,1,0:T(8,128)(2,1)S(1)}, u32[]{:S(2)}, u32[]{:S(2)}) collective-permute-start(bf16[2,112,4864]{2,1,0:T(8,128)(2,1)S(1)} %pad_maximum_fusion.1), channel_id=1, source_target_pairs={{0,8},{1,9},{2,10},{3,11},{4,12},{5,13},{6,14},{7,15}} | collective-permute-start | bytes 6537224 | tf_op jit(solution)/shard_map/ppermute | solution.py:77
  292.7 1.8 copy-start.2
  294.5 1.2 copy-start.13
  294.5 209.9 %all-gather.13.cloned.1.call-start = ((), (), s32[]{:S(2)}) async-start(), calls=%async_computation.3 | async-start | bytes 19611648 | tf_op jit(solution)/shard_map/all_gather | solution.py:80
  295.7 2.9 copy-start.9
  298.6 53.8 %collective-permute-start.4 = (bf16[2,112,4864]{2,1,0:T(8,128)(2,1)S(1)}, bf16[2,112,4864]{2,1,0:T(8,128)(2,1)}, u32[]{:S(2)}, u32[]{:S(2)}) collective-permute-start(bf16[2,112,4864]{2,1,0:T(8,128)(2,1)S(1)} %copy-done.9), channel_id=1, source_target_pairs={{0,8},{1,9},{2,10},{3,11},{4,12},{5,13},{6,14},{7,15}} | collective-permute-start | bytes 6537224 | tf_op jit(solution)/shard_map/ppermute | solution.py:77
  350.6 1.8 copy-start
  352.4 5.1 copy-start.12
  354.1 1.6 copy-start.10
  354.1 210.1 %all-gather.15.cloned.1.call-start = ((), (), s32[]{:S(2)}) async-start(), calls=%async_computation.4 | async-start | bytes 19611648 | tf_op jit(solution)/shard_map/all_gather | solution.py:80
  355.7 46.1 %collective-permute-start.5 = (bf16[2,112,4864]{2,1,0:T(8,128)(2,1)S(1)}, bf16[2,112,4864]{2,1,0:T(8,128)(2,1)S(1)}, u32[]{:S(2)}, u32[]{:S(2)}) collective-permute-start(bf16[2,112,4864]{2,1,0:T(8,128)(2,1)S(1)} %copy-done.10), channel_id=1, source_target_pairs={{0,8},{1,9},{2,10},{3,11},{4,12},{5,13},{6,14},{7,15}} | collective-permute-start | bytes 6537224 | tf_op jit(solution)/shard_map/ppermute | solution.py:77
  403.3 51.1 %copy-start.11 = (bf16[2,112,4864]{2,1,0:T(8,128)(2,1)S(1)}, bf16[2,112,4864]{2,1,0:T(8,128)(2,1)}, u32[]{:S(2)}) copy-start(bf16[2,112,4864]{2,1,0:T(8,128)(2,1)} %pad_maximum_fusion.5) | copy-start | bytes 6537220
  452.5 1.8 copy-start.1
  454.4 200.3 %all-gather.17.cloned.1.call-start = ((), (), s32[]{:S(2)}) async-start(), calls=%async_computation.5 | async-start | bytes 19611648 | tf_op jit(solution)/shard_map/all_gather | solution.py:80
  454.4 48.4 %collective-permute-start.6 = (bf16[2,112,4864]{2,1,0:T(8,128)(2,1)S(1)}, bf16[2,112,4864]{2,1,0:T(8,128)(2,1)S(1)}, u32[]{:S(2)}, u32[]{:S(2)}) collective-permute-start(bf16[2,112,4864]{2,1,0:T(8,128)(2,1)S(1)} %copy-done.11), channel_id=1, source_target_pairs={{0,8},{1,9},{2,10},{3,11},{4,12},{5,13},{6,14},{7,15}} | collective-permute-start | bytes 6537224 | tf_op jit(solution)/shard_map/ppermute | solution.py:77
  553.4 1.8 copy-start.3
  613.5 1.8 copy-start.4
  703.9 82.4 %collective-permute-start.7 = (bf16[2048,896]{1,0:T(8,128)(2,1)S(1)}, bf16[2048,896]{1,0:T(8,128)(2,1)S(1)}, u32[]{:S(2)}, u32[]{:S(2)}) collective-permute-start(bf16[2048,896]{1,0:T(8,128)(2,1)S(1)} %mlp_layer.11), channel_id=1, source_target_pairs={{0,8},{1,9},{2,10},{3,11},{4,12},{5,13},{6,14},{7,15}} | collective-permute-start | bytes 11010056 | tf_op jit(solution)/shard_map/ppermute | solution.py:92
Sparse Core Ops, SparseCore 0:
  98.3 91.3 all-gather.6
  191.5 88.6 all-gather.8
  294.6 88.7 all-gather.10
  385.1 88.6 all-gather.12
  475.5 88.6 all-gather.14
  565.9 88.6 all-gather.16

commit v2 on v1

v2 whole, which is shorter than its diff:
```python
import functools

import jax
import jax.numpy as jnp
from jax import lax
from jax.experimental import pallas as pl
from jax.experimental.pallas import tpu as pltpu
from jax.sharding import PartitionSpec as P

ROOT_2_PI = 0.7978845608
CUBIC = 0.044715 * ROOT_2_PI
MESH = pl.DeviceIdType.MESH
BLOCK = 512
GEN_BLOCKS = 5
Z, X, Y, DIAG, SIB, SIB_X, SIB_Y, SIB_DIAG = range(8)
SLOTS = 8


def gelu(z):
    half = 0.5 * z
    return half + half * jnp.tanh(z * (ROOT_2_PI + CUBIC * (z * z)))


def cuts(total, step):
    return [(at, min(step, total - at)) for at in range(0, total, step)]


def stack_kernel(
    up_ref, down_ref, x_ref, full_ref, y_ref, w_buf, act, h, send, recv, load, x_sem, y_send, y_recv, y_local
):
    layers, piece, ffn = up_ref.shape
    width = x_ref.shape[1]
    tokens = x_ref.shape[0]
    blocks = tokens // BLOCK
    far_blocks = blocks - GEN_BLOCKS
    gen_rows = GEN_BLOCKS * BLOCK
    own_refs = (up_ref, down_ref)
    side = lax.axis_index("side")
    rep = lax.axis_index("rep")
    core = rep % 2
    at_x = (rep // 2) % 2
    at_y = rep // 4
    flip = 1 - 2 * core
    rep_x = rep + 2 - 4 * at_x
    rep_y = rep + 4 - 8 * at_y
    rep_d = rep_y + 2 - 4 * at_x
    is_gen = side == 1
    is_far = side == 0
    to_z = (1 - side, rep)
    to_sib = (side, rep + flip)
    to_x = (side, rep_x)
    to_y = (side, rep_y)
    arrives = (rep, rep_x, rep_y, rep_d, rep + flip, rep_x + flip, rep_y + flip, rep_d + flip)
    my_blocks = GEN_BLOCKS * side + far_blocks * (1 - side)

    def rows(index):
        return pl.ds(pl.multiple_of(index * piece, 16), piece)

    def remote(layer, m, slot, index, target, source=None):
        there = full_ref.at[layer, m, rows(index), :]
        return pltpu.make_async_remote_copy(
            src_ref=there if source is None else source,
            dst_ref=there,
            send_sem=send.at[layer, m, slot],
            recv_sem=recv.at[layer, m, slot],
            device_id=target,
            device_id_type=MESH,
        )

    def fetch(layer, m, slot, source=None):
        where = rows(arrives[slot])
        source = full_ref.at[layer, m, where, :] if source is None else source
        return pltpu.make_async_copy(source, w_buf.at[layer % 2, m, where, :], load.at[layer % 2, m, slot])

    def arrived(layer, m, slot):
        remote(layer, m, slot, arrives[slot], to_sib).wait_recv()
        fetch(layer, m, slot).start()

    def send_z(layer):
        for m in range(2):
            remote(layer, m, Z, rep, to_z, own_refs[m].at[layer]).start()

    def spread(layer, m, source):
        remote(layer, m, X, rep, to_x, source).start()
        remote(layer, m, Y, rep, to_y, source).start()
        remote(layer, m, SIB, rep, to_sib, source).start()

    def send_own(layer, m):
        @pl.when(is_far)
        def _():
            spread(layer, m, own_refs[m].at[layer])

        @pl.when(is_gen)
        def _():
            remote(layer, m, Z, rep, to_z).wait_recv()
            spread(layer, m, None)

    def fetch_own(layer):
        for m in range(2):
            @pl.when(is_far)
            def _():
                fetch(layer, m, Z, own_refs[m].at[layer]).start()

            @pl.when(is_gen)
            def _():
                fetch(layer, m, Z).start()

    def direct(layer, m):
        arrived(layer, m, X)
        if m == 0:
            remote(layer, m, DIAG, rep_x, to_y).start()
        remote(layer, m, SIB_X, rep_x, to_sib).start()
        arrived(layer, m, Y)
        if m == 1:
            remote(layer, m, DIAG, rep_y, to_x).start()
        remote(layer, m, SIB_Y, rep_y, to_sib).start()

    def diagonal(layer, m):
        arrived(layer, m, DIAG)
        remote(layer, m, SIB_DIAG, rep_d, to_sib).start()

    def from_sibling(layer, m):
        for slot in (SIB, SIB_X, SIB_Y, SIB_DIAG):
            arrived(layer, m, slot)

    def far_x():
        return pltpu.make_async_remote_copy(
            src_ref=x_ref.at[pl.ds(gen_rows, far_blocks * BLOCK), :],
            dst_ref=h.at[pl.ds(0, far_blocks * BLOCK), :],
            send_sem=x_sem.at[0],
            recv_sem=x_sem.at[1],
            device_id=to_z,
            device_id_type=MESH,
        )

    def near_x():
        return pltpu.make_async_copy(x_ref.at[pl.ds(0, gen_rows), :], h.at[...], x_sem.at[2])

    def far_y(b):
        return pltpu.make_async_remote_copy(
            src_ref=h.at[pl.ds(pl.multiple_of(b * BLOCK, BLOCK), BLOCK), :],
            dst_ref=y_ref.at[pl.ds(pl.multiple_of(gen_rows + b * BLOCK, BLOCK), BLOCK), :],
            send_sem=y_send.at[b],
            recv_sem=y_recv.at[b],
            device_id=to_z,
            device_id_type=MESH,
        )

    def near_y(b):
        where = pl.ds(pl.multiple_of(b * BLOCK, BLOCK), BLOCK)
        return pltpu.make_async_copy(h.at[where, :], y_ref.at[where, :], y_local.at[b])

    def compute(layer, b):
        par = layer % 2
        where = pl.ds(pl.multiple_of(b * BLOCK, BLOCK), BLOCK)
        h_block = h[where, :]
        for at, size in cuts(ffn, 512):
            z = jnp.dot(h_block, w_buf[par, 0, :, at : at + size], preferred_element_type=jnp.float32)
            act[:, at : at + size] = gelu(z).astype(jnp.bfloat16)
        for at, size in cuts(width, 256):
            p = lax.dot_general(
                act[...],
                w_buf[par, 1, at : at + size, :],
                (((1,), (1,)), ((), ())),
                preferred_element_type=jnp.float32,
            )
            h[where, at : at + size] = (h[where, at : at + size].astype(jnp.float32) + p).astype(jnp.bfloat16)

    barrier = pltpu.get_barrier_semaphore()
    for target in (to_z, to_sib, to_x, to_y):
        pl.semaphore_signal(barrier, inc=1, device_id=target, device_id_type=MESH)
    pl.semaphore_wait(barrier, 4)

    @pl.when(is_far)
    def _():
        send_z(0)

    @pl.when(is_gen)
    def _():
        far_x().start()
        near_x().start()

    send_own(0, 0)
    send_own(0, 1)

    def step(s, carry):
        receiving = s < layers

        @pl.when(receiving)
        def _():
            fetch_own(s)

        @pl.when(is_far & (s + 1 < layers))
        def _():
            send_z(s + 1)

        @pl.when(is_far & (s == 1))
        def _():
            far_x().wait_recv()

        @pl.when(is_gen & (s == 1))
        def _():
            near_x().wait()

        def block(b, inner):
            @pl.when((s > 0) & (b < my_blocks))
            def _():
                compute(s - 1, b)

            @pl.when((s == layers) & (b < my_blocks) & is_gen)
            def _():
                near_y(b).start()

            @pl.when((s == layers) & (b < my_blocks) & is_far)
            def _():
                far_y(b).start()

            @pl.when(receiving & (b == 1))
            def _():
                direct(s, 0)

            @pl.when(receiving & (b == 3))
            def _():
                direct(s, 1)

            @pl.when((s + 1 < layers) & (b == 3))
            def _():
                send_own(s + 1, 0)
                send_own(s + 1, 1)

            @pl.when(receiving & (b == 4))
            def _():
                for m in range(2):
                    diagonal(s, m)
                for m in range(2):
                    from_sibling(s, m)

            return inner

        lax.fori_loop(0, GEN_BLOCKS, block, 0)

        @pl.when(receiving)
        def _():
            for m in range(2):
                for slot in range(SLOTS):
                    fetch(s, m, slot).wait()

        return carry

    lax.fori_loop(0, layers + 1, step, 0)

    @pl.when(is_gen)
    def _():
        far_x().wait_send()
        for b in range(GEN_BLOCKS):
            near_y(b).wait()
        for b in range(far_blocks):
            far_y(b).wait_recv()

    @pl.when(is_far)
    def _():
        for b in range(far_blocks):
            far_y(b).wait_send()

    def drain(layer, carry):
        for m in range(2):
            @pl.when(is_far)
            def _():
                remote(layer, m, Z, rep, to_z).wait_send()

            for slot in range(1, SLOTS):
                remote(layer, m, slot, rep, to_sib).wait_send()
        return carry

    lax.fori_loop(0, layers, drain, 0)


def mlp_stack(up, down, x):
    layers, piece, ffn = up.shape
    tokens, width = x.shape
    hbm = pl.BlockSpec(memory_space=pltpu.HBM)
    dma = pltpu.SemaphoreType.DMA
    _, y = pl.pallas_call(
        stack_kernel,
        in_specs=[hbm] * 3,
        out_specs=[hbm] * 2,
        out_shape=[
            jax.ShapeDtypeStruct((layers, 2, width, ffn), jnp.bfloat16),
            jax.ShapeDtypeStruct((tokens, width), jnp.bfloat16),
        ],
        scratch_shapes=[
            pltpu.VMEM((2, 2, width, ffn), jnp.bfloat16),
            pltpu.VMEM((BLOCK, ffn), jnp.bfloat16),
            pltpu.VMEM((GEN_BLOCKS * BLOCK, width), jnp.bfloat16),
            dma((layers, 2, SLOTS)),
            dma((layers, 2, SLOTS)),
            dma((2, 2, SLOTS)),
            dma((3,)),
            dma((GEN_BLOCKS,)),
            dma((GEN_BLOCKS,)),
            dma((GEN_BLOCKS,)),
        ],
        compiler_params=pltpu.CompilerParams(
            collective_id=0, has_side_effects=True, vmem_limit_bytes=60 * 2**20
        ),
        name="mlp_stack",
    )(up, down, x)
    return y


def solution(mesh):
    up_spec = P("side", None, "rep", None)
    down_spec = P("side", None, None, "rep")
    act_spec = P("side", "rep", None)

    def device_step(w_up, w_down, g_up, g_down, learn_rate, prompts, prompt_lens):
        is_gen = lax.axis_index("side") == 1
        tokens = prompts.shape[1]
        new_up = w_up - learn_rate * g_up
        new_down = w_down - learn_rate * g_down
        up_bf = new_up[0].astype(jnp.bfloat16)
        down_bf = jnp.swapaxes(new_down[0], 1, 2).astype(jnp.bfloat16)
        out = mlp_stack(up_bf, down_bf, prompts[0])
        keep = (jnp.arange(tokens)[:, None] < prompt_lens[0]) & is_gen
        out = jnp.where(keep, out, jnp.zeros_like(out))
        return new_up, new_down, out[None]

    return jax.shard_map(
        device_step,
        mesh=mesh,
        in_specs=(up_spec, down_spec, up_spec, down_spec, P(), act_spec, P("rep")),
        out_specs=(up_spec, down_spec, act_spec),
        check_vma=False,
    )
```

time: 803 us -> 567 us (0.71)
  the two profiles are of different devices: /device:TPU:0 before, /device:TPU:11 now
where the time goes in v2:
time: 567 us
  Pallas kernels  528 us (93%)
  other arithmetic  35.5 us (6%)
    pallas_call x1, Pallas kernels, mlp_stack(): pl.pallas_call(stack_kernel, in_specs=[hbm] * 3, out_specs=[hbm] * 2, out...  528 us
    convert_element_type x1, other arithmetic, device_step(): up_bf = new_up[0].astype(jnp.bfloat16)  17.2 us
    convert_element_type x1, other arithmetic, device_step(): down_bf = jnp.swapaxes(new_down[0], 1, 2).astype(jnp.bfloat16)  11.4 us

profile of v2, /device:TPU:11, one launch (start us, length us, event | category | flops | bytes accessed | tf_op | source)
XLA Modules:
  0.0 566.9 jit_solution(12771560470588891857)
XLA Ops:
  1.3 0.0 copy-start
  1.3 17.2 %convert_bitcast_fusion.1 = (bf16[6,112,4864]{2,1,0:T(8,128)(2,1)}, f32[1,6,112,4864]{3,2,1,0:T(8,128)}) fusion(f32[1,6,112,4864]{3,2,1,0:T(8,128)} %param.7, f32[1,6,112,4864]{3,2,1,0:T(8,128)} %param.9, f32[]{:T(128)S(6)} %copy.10), kind=kLoop, calls=%fused_computation.4 | loop fusion | flops 9805824 | bytes 45760516 | tf_op jit(solution)/shard_map/convert_element_type | solution.py:321
  18.5 1.9 copy-done
  20.4 11.4 %convert_bitcast_fusion = (bf16[6,112,4864]{2,1,0:T(8,128)(2,1)}, f32[1,6,4864,112]{2,3,1,0:T(8,128)}) fusion(f32[1,6,4864,112]{2,3,1,0:T(8,128)S(1)} %copy-done, f32[1,6,4864,112]{2,3,1,0:T(8,128)} %param.10, f32[]{:T(128)S(6)} %copy.10), kind=kLoop, calls=%fused_computation.3 | loop fusion | flops 9805824 | bytes 45760516 | tf_op jit(solution)/shard_map/convert_element_type | solution.py:322
  31.8 527.6 %mlp_stack.1 = (bf16[6,2,896,4864]{3,2,1,0:T(8,128)(2,1)}, bf16[4096,896]{1,0:T(8,128)(2,1)}) custom-call(bf16[6,112,4864]{2,1,0:T(8,128)(2,1)} %get-tuple-element.7.up_ref, bf16[6,112,4864]{2,1,0:T(8,128)(2,1)} %get-tuple-element.5.down_ref, bf16[4096,896]{1,0:T(8,128)(2,1)} %bitcast.11), custom_call_target="tpu_custom_call" | custom-call | tf_op jit(solution)/shard_map/mlp_stack/pallas_call | solution.py:283
  560.1 6.8 %select_bitcast_fusion = bf16[1,4096,896]{2,1,0:T(8,128)(2,1)} fusion(bf16[4096,896]{1,0:T(8,128)(2,1)} %get-tuple-element.4, pred[4096]{0:T(1024)(128)(4,1)S(1)} %fusion), kind=kLoop, calls=%fused_computation.2 | loop fusion | flops 3670016 | bytes 14684160 | tf_op jit(solution)/shard_map/broadcast_in_dim | solution.py:326
  (1 shorter events, 0.0 us)
Async XLA Ops:
  1.3 19.1 %copy-start = (f32[1,6,4864,112]{2,3,1,0:T(8,128)S(1)}, f32[1,6,4864,112]{2,3,1,0:T(8,128)}, u32[]{:S(2)}) copy-start(f32[1,6,4864,112]{2,3,1,0:T(8,128)} %param.8) | copy-start | bytes 39223300

commit v3 on v2

v3 whole, which is shorter than its diff:
```python
import functools

import jax
import jax.numpy as jnp
from jax import lax
from jax.experimental import pallas as pl
from jax.experimental.pallas import tpu as pltpu
from jax.sharding import PartitionSpec as P

ROOT_2_PI = 0.7978845608
CUBIC = 0.044715 * ROOT_2_PI
MESH = pl.DeviceIdType.MESH
BLOCK = 256
GEN_BLOCKS = 10
HANDED = 2
DIRECT_AT = (0, 2)
OWN_AT = (0, 2)
DIAG_AT = 8
SIB_AT = 9
Z_AHEAD = 2
PARTS = 2
Z, X, Y, DIAG, SIB, SIB_X, SIB_Y, SIB_DIAG = range(8)
SLOTS = 8


def gelu(z):
    half = 0.5 * z
    return half + half * jnp.tanh(z * (ROOT_2_PI + CUBIC * (z * z)))


def cuts(total, step):
    return [(at, min(step, total - at)) for at in range(0, total, step)]


def stack_kernel(
    up_ref, down_ref, first_ref, x_ref, full_ref, y_ref, w_buf, act, acc, h, send, recv, load, x_sem, hand_send, hand_recv, y_send, y_recv, y_local
):
    steps, _, width, ffn = full_ref.shape
    piece = up_ref.shape[1]
    tokens = x_ref.shape[0]
    blocks = tokens // BLOCK
    far_blocks = blocks - GEN_BLOCKS
    gen_rows = GEN_BLOCKS * BLOCK
    own_refs = (up_ref, down_ref)
    side = lax.axis_index("side")
    rep = lax.axis_index("rep")
    core = rep % 2
    at_x = (rep // 2) % 2
    at_y = rep // 4
    flip = 1 - 2 * core
    rep_x = rep + 2 - 4 * at_x
    rep_y = rep + 4 - 8 * at_y
    rep_d = rep_y + 2 - 4 * at_x
    is_gen = side == 1
    is_far = side == 0
    to_z = (1 - side, rep)
    to_sib = (side, rep + flip)
    to_x = (side, rep_x)
    to_y = (side, rep_y)
    arrives = (rep, rep_x, rep_y, rep_d, rep + flip, rep_x + flip, rep_y + flip, rep_d + flip)
    my_blocks = GEN_BLOCKS * side + far_blocks * (1 - side)
    all_blocks = GEN_BLOCKS + HANDED

    def rows(index):
        return pl.ds(pl.multiple_of(index * piece, 16), piece)

    def remote(turn, m, slot, index, target, source=None):
        there = full_ref.at[turn, m, rows(index), :]
        return pltpu.make_async_remote_copy(
            src_ref=there if source is None else source,
            dst_ref=there,
            send_sem=send.at[turn, m, slot],
            recv_sem=recv.at[turn, m, slot],
            device_id=target,
            device_id_type=MESH,
        )

    def own(turn, m):
        columns = pl.ds(pl.multiple_of(turn % PARTS * ffn, 128), ffn)
        return own_refs[m].at[turn // PARTS, :, columns]

    def fetch(turn, m, slot, source=None):
        where = rows(arrives[slot])
        source = full_ref.at[turn, m, where, :] if source is None else source
        return pltpu.make_async_copy(source, w_buf.at[turn % 2, m, where, :], load.at[turn % 2, m, slot])

    def received(turn, m, slot):
        remote(turn, m, slot, arrives[slot], to_sib).wait_recv()

    def arrived(turn, m, slot):
        received(turn, m, slot)
        fetch(turn, m, slot).start()

    def send_z(turn):
        for m in range(2):
            remote(turn, m, Z, rep, to_z, own(turn, m)).start()

    def spread(turn, m, source):
        remote(turn, m, X, rep, to_x, source).start()
        remote(turn, m, Y, rep, to_y, source).start()
        remote(turn, m, SIB, rep, to_sib, source).start()

    def send_own(turn, m, first=False):
        @pl.when(is_far)
        def _():
            spread(turn, m, own(turn, m))

        @pl.when(is_gen)
        def _():
            if first:
                spread(turn, m, first_ref.at[m])
            else:
                received(turn, m, Z)
                spread(turn, m, None)

    def fetch_own(turn):
        for m in range(2):
            @pl.when(is_far)
            def _():
                fetch(turn, m, Z, own(turn, m)).start()

            @pl.when(is_gen & (turn == 0))
            def _():
                fetch(turn, m, Z, first_ref.at[m]).start()

            @pl.when(is_gen & (turn > 0))
            def _():
                fetch(turn, m, Z).start()

    def direct(turn, m):
        received(turn, m, X)
        if m == 0:
            remote(turn, m, DIAG, rep_x, to_y).start()
        remote(turn, m, SIB_X, rep_x, to_sib).start()
        received(turn, m, Y)
        if m == 1:
            remote(turn, m, DIAG, rep_y, to_x).start()
        remote(turn, m, SIB_Y, rep_y, to_sib).start()

    def diagonal(turn, m):
        fetch(turn, m, X).start()
        fetch(turn, m, Y).start()
        arrived(turn, m, DIAG)
        remote(turn, m, SIB_DIAG, rep_d, to_sib).start()

    def from_sibling(turn, m):
        for slot in (SIB, SIB_X, SIB_Y, SIB_DIAG):
            arrived(turn, m, slot)

    def far_x():
        return pltpu.make_async_remote_copy(
            src_ref=x_ref.at[pl.ds(gen_rows, far_blocks * BLOCK), :],
            dst_ref=h.at[pl.ds(0, far_blocks * BLOCK), :],
            send_sem=x_sem.at[0],
            recv_sem=x_sem.at[1],
            device_id=to_z,
            device_id_type=MESH,
        )

    def near_x():
        return pltpu.make_async_copy(x_ref.at[pl.ds(0, gen_rows), :], h.at[pl.ds(0, gen_rows), :], x_sem.at[2])

    def hand(b):
        return pltpu.make_async_remote_copy(
            src_ref=h.at[pl.ds(pl.multiple_of(b * BLOCK, BLOCK), BLOCK), :],
            dst_ref=h.at[pl.ds(pl.multiple_of(gen_rows + b * BLOCK, BLOCK), BLOCK), :],
            send_sem=hand_send.at[b],
            recv_sem=hand_recv.at[b],
            device_id=to_z,
            device_id_type=MESH,
        )

    def far_y(b):
        return pltpu.make_async_remote_copy(
            src_ref=h.at[pl.ds(pl.multiple_of(b * BLOCK, BLOCK), BLOCK), :],
            dst_ref=y_ref.at[pl.ds(pl.multiple_of(gen_rows + b * BLOCK, BLOCK), BLOCK), :],
            send_sem=y_send.at[b],
            recv_sem=y_recv.at[b],
            device_id=to_z,
            device_id_type=MESH,
        )

    def near_y(b):
        where = pl.ds(pl.multiple_of(b * BLOCK, BLOCK), BLOCK)
        return pltpu.make_async_copy(h.at[where, :], y_ref.at[where, :], y_local.at[b])

    def compute(turn, b, part):
        par = turn % 2
        where = pl.ds(pl.multiple_of(b * BLOCK, BLOCK), BLOCK)
        h_block = h[where, :]
        for at, size in cuts(ffn, 512):
            z = jnp.dot(h_block, w_buf[par, 0, :, at : at + size], preferred_element_type=jnp.float32)
            act[:, at : at + size] = gelu(z).astype(jnp.bfloat16)
        for at, size in cuts(width, 256):
            p = lax.dot_general(
                act[...],
                w_buf[par, 1, at : at + size, :],
                (((1,), (1,)), ((), ())),
                preferred_element_type=jnp.float32,
            )
            if part < PARTS - 1:
                acc[where, at : at + size] = p if part == 0 else acc[where, at : at + size] + p
            else:
                p = acc[where, at : at + size] + p
                h[where, at : at + size] = (h[where, at : at + size].astype(jnp.float32) + p).astype(jnp.bfloat16)

    barrier = pltpu.get_barrier_semaphore()
    for target in (to_z, to_sib, to_x, to_y):
        pl.semaphore_signal(barrier, inc=1, device_id=target, device_id_type=MESH)
    pl.semaphore_wait(barrier, 4)

    @pl.when(is_far)
    def _():
        for ahead in range(1, Z_AHEAD):
            send_z(ahead)

    @pl.when(is_gen)
    def _():
        far_x().start()
        near_x().start()

    send_own(0, 0, True)
    send_own(0, 1, True)

    def step(s, carry):
        ready = s
        done = s - 1
        receiving = s < steps
        closing = receiving
        last = done == steps - 1
        tail = jnp.where(done >= steps - PARTS, HANDED, 0)
        low = tail * (1 - side)
        high = my_blocks + tail * side

        @pl.when(closing)
        def _():
            fetch_own(ready)

        @pl.when(is_far & (s + Z_AHEAD < steps))
        def _():
            send_z(s + Z_AHEAD)

        @pl.when(is_far & (done == 0))
        def _():
            far_x().wait_recv()

        @pl.when(is_gen & (done == 0))
        def _():
            near_x().wait()

        def block(b, inner):
            for m in range(2):
                @pl.when(receiving & (b == DIRECT_AT[m]))
                def _():
                    direct(s, m)

                @pl.when((s + 1 < steps) & (b == OWN_AT[m]))
                def _():
                    send_own(s + 1, m)

            @pl.when(closing & (b == DIAG_AT))
            def _():
                for m in range(2):
                    diagonal(ready, m)

            @pl.when(closing & (b == SIB_AT))
            def _():
                for m in range(2):
                    from_sibling(ready, m)

            mine = (b >= low) & (b < high)

            @pl.when(is_gen & (done == steps - PARTS) & mine & (b >= GEN_BLOCKS))
            def _():
                hand(b - GEN_BLOCKS).wait_recv()

            for part in range(PARTS):
                @pl.when((done >= 0) & (done % PARTS == part) & mine)
                def _():
                    compute(done, b, part)

            @pl.when(is_far & (done == steps - PARTS - 1) & (b < HANDED))
            def _():
                hand(b).start()

            @pl.when(last & mine & is_gen)
            def _():
                near_y(b).start()

            @pl.when(last & mine & is_far)
            def _():
                far_y(b).start()

            return inner

        lax.fori_loop(0, all_blocks, block, 0)

        @pl.when(closing)
        def _():
            for m in range(2):
                for slot in range(SLOTS):
                    fetch(ready, m, slot).wait()

        return carry

    lax.fori_loop(0, steps + 1, step, 0)

    @pl.when(is_gen)
    def _():
        far_x().wait_send()
        for b in range(all_blocks):
            near_y(b).wait()
        for b in range(HANDED, far_blocks):
            far_y(b).wait_recv()

    @pl.when(is_far)
    def _():
        for b in range(HANDED):
            hand(b).wait_send()
        for b in range(HANDED, far_blocks):
            far_y(b).wait_send()

    def drain(turn, carry):
        for m in range(2):
            @pl.when(is_far & (turn > 0))
            def _():
                remote(turn, m, Z, rep, to_z).wait_send()

            for slot in range(1, SLOTS):
                remote(turn, m, slot, rep, to_sib).wait_send()
        return carry

    lax.fori_loop(0, steps, drain, 0)


def mlp_stack(up, down, first, x):
    layers, piece, ffn = up.shape
    tokens, width = x.shape
    steps, ffn = layers * PARTS, ffn // PARTS
    hbm = pl.BlockSpec(memory_space=pltpu.HBM)
    dma = pltpu.SemaphoreType.DMA
    _, y = pl.pallas_call(
        stack_kernel,
        in_specs=[hbm] * 4,
        out_specs=[hbm] * 2,
        out_shape=[
            jax.ShapeDtypeStruct((steps, 2, width, ffn), jnp.bfloat16),
            jax.ShapeDtypeStruct((tokens, width), jnp.bfloat16),
        ],
        scratch_shapes=[
            pltpu.VMEM((2, 2, width, ffn), jnp.bfloat16),
            pltpu.VMEM((BLOCK, ffn), jnp.bfloat16),
            pltpu.VMEM(((GEN_BLOCKS + HANDED) * BLOCK, width), jnp.float32),
            pltpu.VMEM(((GEN_BLOCKS + HANDED) * BLOCK, width), jnp.bfloat16),
            dma((steps, 2, SLOTS)),
            dma((steps, 2, SLOTS)),
            dma((2, 2, SLOTS)),
            dma((3,)),
            dma((HANDED,)),
            dma((HANDED,)),
            dma((tokens // BLOCK,)),
            dma((tokens // BLOCK,)),
            dma((tokens // BLOCK,)),
        ],
        compiler_params=pltpu.CompilerParams(
            collective_id=0, has_side_effects=True, vmem_limit_bytes=60 * 2**20
        ),
        name="mlp_stack",
    )(up, down, first, x)
    return y


def solution(mesh):
    up_spec = P("side", None, "rep", None)
    down_spec = P("side", None, None, "rep")
    act_spec = P("side", "rep", None)

    def device_step(w_up, w_down, g_up, g_down, learn_rate, prompts, prompt_lens):
        is_gen = lax.axis_index("side") == 1
        tokens = prompts.shape[1]
        part = w_up.shape[3] // PARTS
        first_up = w_up[0, 0, :, :part] - learn_rate * g_up[0, 0, :, :part]
        first_down = (w_down[0, 0, :part] - learn_rate * g_down[0, 0, :part]).T
        first = jnp.stack([first_up.astype(jnp.bfloat16), first_down.astype(jnp.bfloat16)])
        first, w_up, w_down = lax.optimization_barrier((first, w_up, w_down))
        first = lax.ppermute(first, "side", [(0, 1)])
        new_up = w_up - learn_rate * g_up
        new_down = w_down - learn_rate * g_down
        up_bf = new_up[0].astype(jnp.bfloat16)
        down_bf = jnp.swapaxes(new_down[0], 1, 2).astype(jnp.bfloat16)
        out = mlp_stack(up_bf, down_bf, first, prompts[0])
        keep = (jnp.arange(tokens)[:, None] < prompt_lens[0]) & is_gen
        out = jnp.where(keep, out, jnp.zeros_like(out))
        return new_up, new_down, out[None]

    return jax.shard_map(
        device_step,
        mesh=mesh,
        in_specs=(up_spec, down_spec, up_spec, down_spec, P(), act_spec, P("rep")),
        out_specs=(up_spec, down_spec, act_spec),
        check_vma=False,
    )
```

time: 567 us -> 535 us (0.944)
  the two profiles are of different devices: /device:TPU:11 before, /device:TPU:0 now
where the time goes in v3:
time: 535 us; the launch traced here: 529 us
  Pallas kernels  478 us (89%)
  other arithmetic  43.5 us (8%)
    pallas_call x1, Pallas kernels, mlp_stack(): pl.pallas_call(stack_kernel, in_specs=[hbm] * 4, out_specs=[hbm] * 2, out...  478 us
    convert_element_type x1, other arithmetic, device_step(): down_bf = jnp.swapaxes(new_down[0], 1, 2).astype(jnp.bfloat16)  16.6 us
    convert_element_type x1, other arithmetic, device_step(): up_bf = new_up[0].astype(jnp.bfloat16)  16.6 us
  transfers between devices with their start and end apart: 1, of which 0 were waited for; matrix products, arithmetic and copies ran while one was open for 6% of the time, Pallas kernels for 0%

profile of v3, /device:TPU:0, one launch (start us, length us, event | category | flops | bytes accessed | tf_op | source)
XLA Modules:
  0.0 529.4 jit_solution(10818671091922312286)
XLA Ops:
  1.3 1.7 fusion.1
  3.0 1.7 fusion
  4.6 0.1 pad_maximum_fusion
  4.8 5.3 collective-permute-start
  10.1 16.6 %convert_bitcast_fusion.1 = (bf16[6,112,4864]{2,1,0:T(8,128)(2,1)}, f32[1,6,112,4864]{3,2,1,0:T(8,128)}) fusion(f32[1,6,112,4864]{3,2,1,0:T(8,128)} %param.7, f32[1,6,112,4864]{3,2,1,0:T(8,128)} %param.9, f32[]{:T(128)S(6)} %copy.10), kind=kLoop, calls=%fused_computation.4 | loop fusion | flops 9805824 | bytes 45760516 | tf_op jit(solution)/shard_map/convert_element_type | solution.py:389
  27.3 16.6 %convert_bitcast_fusion = (bf16[6,112,4864]{2,1,0:T(8,128)(2,1)}, f32[1,6,4864,112]{2,3,1,0:T(8,128)}) fusion(f32[1,6,4864,112]{2,3,1,0:T(8,128)} %param.8, f32[1,6,4864,112]{2,3,1,0:T(8,128)} %param.10, f32[]{:T(128)S(6)} %copy.10), kind=kLoop, calls=%fused_computation.3 | loop fusion | flops 9805824 | bytes 45760516 | tf_op jit(solution)/shard_map/convert_element_type | solution.py:390
  43.9 0.0 collective-permute-done.first_ref
  43.9 0.0 copy-start
  43.9 1.0 copy-done
  44.9 477.7 %mlp_stack.1 = (bf16[12,2,896,2432]{3,2,1,0:T(8,128)(2,1)}, bf16[4096,896]{1,0:T(8,128)(2,1)}) custom-call(bf16[6,112,4864]{2,1,0:T(8,128)(2,1)} %get-tuple-element.13.up_ref, bf16[6,112,4864]{2,1,0:T(8,128)(2,1)} %get-tuple-element.11.down_ref, bf16[2,112,2432]{2,1,0:T(8,128)(2,1)} %copy-done, bf16[4096,896]{1,0:T(8,128)(2,1)} %bitcast.19), custom_call_target="tpu_custom_call" | custom-call | tf_op jit(solution)/shard_map/mlp_stack/pallas_call | solution.py:342
  522.6 6.8 %select_bitcast_fusion = bf16[1,4096,896]{2,1,0:T(8,128)(2,1)} fusion(bf16[4096,896]{1,0:T(8,128)(2,1)} %get-tuple-element.10, pred[4096]{0:T(1024)(128)(4,1)S(1)} %fusion.2), kind=kLoop, calls=%fused_computation.2 | loop fusion | flops 3670016 | bytes 14684160 | tf_op jit(solution)/shard_map/broadcast_in_dim | solution.py:394
  (1 shorter events, 0.0 us)
Async XLA Ops:
  4.8 39.2 %collective-permute-start = (bf16[2,112,2432]{2,1,0:T(8,128)(2,1)S(1)}, bf16[2,112,2432]{2,1,0:T(8,128)(2,1)S(1)}, u32[]{:S(2)}, u32[]{:S(2)}) collective-permute-start(bf16[2,112,2432]{2,1,0:T(8,128)(2,1)S(1)} %pad_maximum_fusion), channel_id=1, source_target_pairs={{0,8},{1,9},{2,10},{3,11},{4,12},{5,13},{6,14},{7,15}} | collective-permute-start | bytes 3268616 | tf_op jit(solution)/shard_map/ppermute | solution.py:386
  43.9 1.0 copy-start

commit v4 on v3

--- a/solution.py
+++ b/solution.py
@@ -13,9 +13,9 @@
 BLOCK = 256
 GEN_BLOCKS = 10
 HANDED = 2
-DIRECT_AT = (0, 2)
-OWN_AT = (0, 2)
-DIAG_AT = 8
+DIRECT_AT = (1, 3)
+OWN_AT = (1, 3)
+DIAG_AT = 9
 SIB_AT = 9
 Z_AHEAD = 2
 PARTS = 2
@@ -331,6 +331,32 @@
         return carry
 
     lax.fori_loop(0, steps, drain, 0)
+
+
+def update_kernel(rate_ref, w_up, g_up, w_down, g_down, new_up, new_down, up_bf, down_bf):
+    rate = rate_ref[0]
+    for w, g, new, rounded in ((w_up, g_up, new_up, up_bf), (w_down, g_down, new_down, down_bf)):
+        value = w[...] - rate * g[...]
+        new[...] = value
+        rounded[...] = value.astype(jnp.bfloat16)
+
+
+def update(rate, *arrays):
+    layers, piece, ffn = arrays[0].shape
+    block = pl.BlockSpec((1, piece, ffn // PARTS), lambda layer, part: (layer, 0, part))
+    kinds = (jnp.float32, jnp.float32, jnp.bfloat16, jnp.bfloat16)
+    return pl.pallas_call(
+        update_kernel,
+        grid=(layers, PARTS),
+        in_specs=[pl.BlockSpec(memory_space=pltpu.SMEM)] + [block] * 4,
+        out_specs=[block] * 4,
+        out_shape=[jax.ShapeDtypeStruct((layers, piece, ffn), kind) for kind in kinds],
+        compiler_params=pltpu.CompilerParams(vmem_limit_bytes=62 * 2**20),
+        cost_estimate=pl.CostEstimate(
+            flops=60 * layers * piece * ffn, bytes_accessed=28 * layers * piece * ffn, transcendentals=0
+        ),
+        name="update",
+    )(rate.reshape(1), *arrays)
 
 
 def mlp_stack(up, down, first, x):
@@ -384,14 +410,13 @@
         first = jnp.stack([first_up.astype(jnp.bfloat16), first_down.astype(jnp.bfloat16)])
         first, w_up, w_down = lax.optimization_barrier((first, w_up, w_down))
         first = lax.ppermute(first, "side", [(0, 1)])
-        new_up = w_up - learn_rate * g_up
-        new_down = w_down - learn_rate * g_down
-        up_bf = new_up[0].astype(jnp.bfloat16)
-        down_bf = jnp.swapaxes(new_down[0], 1, 2).astype(jnp.bfloat16)
+        new_up, new_down, up_bf, down_bf = update(
+            learn_rate, w_up[0], g_up[0], jnp.swapaxes(w_down[0], 1, 2), jnp.swapaxes(g_down[0], 1, 2)
+        )
         out = mlp_stack(up_bf, down_bf, first, prompts[0])
         keep = (jnp.arange(tokens)[:, None] < prompt_lens[0]) & is_gen
         out = jnp.where(keep, out, jnp.zeros_like(out))
-        return new_up, new_down, out[None]
+        return new_up[None], jnp.swapaxes(new_down, 1, 2)[None], out[None]
 
     return jax.shard_map(
         device_step,

time: 535 us -> 532 us (level)
  other arithmetic: 43.5 us -> 11.3 us
  Pallas kernels: 478 us -> 508 us
    convert_element_type x2 -> x0, other arithmetic: 33.2 us -> none  [the longest x1 16.6 us: device_step(): down_bf = jnp.swapaxes(new_down[0], 1, 2).astype(jnp.bfloat16)]
    pallas_call x0 -> x1, Pallas kernels: none -> 30.3 us  [update(): pl.pallas_call(update_kernel, grid=(layers, PARTS), in_specs=[pl.BlockSpe...]
  transfers between devices with their start and end apart: 1 -> 1, of which waited for: 0 -> 0; matrix products, arithmetic and copies ran while one was open for 6% -> 0% of each run, Pallas kernels for 0% -> 6%
where the time goes in v4:
time: 532 us; the launch traced here: 528 us
  Pallas kernels  508 us (95%)
  other arithmetic  11.3 us (2%)
    pallas_call x1, Pallas kernels, mlp_stack(): pl.pallas_call(stack_kernel, in_specs=[hbm] * 4, out_specs=[hbm] * 2, out...  478 us
    pallas_call x1, Pallas kernels, update(): pl.pallas_call(update_kernel, grid=(layers, PARTS), in_specs=[pl.BlockSpe...  30.3 us
  transfers between devices with their start and end apart: 1, of which 0 were waited for; matrix products, arithmetic and copies ran while one was open for 0% of the time, Pallas kernels for 6%

profile of v4, /device:TPU:0, one launch (start us, length us, event | category | flops | bytes accessed | tf_op | source)
XLA Modules:
  0.0 527.8 jit_solution(6522496683769321515)
XLA Ops:
  1.3 1.7 fusion.1
  3.0 1.7 fusion
  4.6 1.1 pad_maximum_fusion
  5.7 5.3 collective-permute-start
  11.7 30.3 %update.1 = (f32[6,112,4864]{2,1,0:T(8,128)}, f32[6,112,4864]{2,1,0:T(8,128)}, bf16[6,112,4864]{2,1,0:T(8,128)(2,1)}, bf16[6,112,4864]{2,1,0:T(8,128)(2,1)}) custom-call(f32[1]{0:T(128)} %bitcast.25.rate_ref, f32[6,112,4864]{2,1,0:T(8,128)} %bitcast.27, f32[6,112,4864]{2,1,0:T(8,128)} %bitcast.28, f32[6,112,4864]{2,1,0:T(8,128)} %bitcast.29, ...), custom_call_target="tpu_custom_call" | custom-call | flops 196116480 | bytes 91521024 | tf_op jit(solution)/shard_map/update/pallas_call | solution.py:348
  42.0 0.0 collective-permute-done.first_ref
  42.0 0.0 copy-start
  42.0 1.0 copy-done
  42.9 478.0 %mlp_stack.1 = (bf16[12,2,896,2432]{3,2,1,0:T(8,128)(2,1)}, bf16[4096,896]{1,0:T(8,128)(2,1)}) custom-call(bf16[6,112,4864]{2,1,0:T(8,128)(2,1)} %get-tuple-element.15.up_ref, bf16[6,112,4864]{2,1,0:T(8,128)(2,1)} %get-tuple-element.16.down_ref, bf16[2,112,2432]{2,1,0:T(8,128)(2,1)} %copy-done, bf16[4096,896]{1,0:T(8,128)(2,1)} %bitcast.31), custom_call_target="tpu_custom_call" | custom-call | tf_op jit(solution)/shard_map/mlp_stack/pallas_call | solution.py:368
  521.0 6.8 %select_bitcast_fusion = bf16[1,4096,896]{2,1,0:T(8,128)(2,1)} fusion(bf16[4096,896]{1,0:T(8,128)(2,1)} %get-tuple-element.18, pred[4096]{0:T(1024)(128)(4,1)S(1)} %fusion.2), kind=kLoop, calls=%fused_computation | loop fusion | flops 3670016 | bytes 14684160 | tf_op jit(solution)/shard_map/broadcast_in_dim | solution.py:419
  (1 shorter events, 0.0 us)
Async XLA Ops:
  5.7 36.2 %collective-permute-start = (bf16[2,112,2432]{2,1,0:T(8,128)(2,1)}, bf16[2,112,2432]{2,1,0:T(8,128)(2,1)S(1)}, u32[]{:S(2)}, u32[]{:S(2)}) collective-permute-start(bf16[2,112,2432]{2,1,0:T(8,128)(2,1)} %pad_maximum_fusion), channel_id=1, source_target_pairs={{0,8},{1,9},{2,10},{3,11},{4,12},{5,13},{6,14},{7,15}} | collective-permute-start | bytes 3268616 | tf_op jit(solution)/shard_map/ppermute | solution.py:412
  42.0 1.0 copy-start
